TPU v7x, 32 devices: a whole 2x2x4 slice. The times are simulated.
32 devices in a mesh: dp: 16 (over z, y, core), space: 2 (over x).
Axes of the slice: x: 2, y: 2, z: 4, core: 2. Of those that a mesh axis runs over, the one named last changes fastest.
Arguments:
- images: bfloat16 [16, 3, 512, 512], P('dp', None, 'space'), may hold values from -6 to 6
- pos_embed: bfloat16 [1024, 1280], P('space'), may hold values from -3 to 3
- conv_first: bfloat16 [3, 3, 3, 64], replicated, may hold values from -1.75 to 1.75
- conv_second: bfloat16 [3, 3, 64, 128], replicated, may hold values from -0.375 to 0.375
- conv_third: bfloat16 [3, 3, 128, 256], replicated, may hold values from -0.25 to 0.25
- conv_fourth: bfloat16 [3, 3, 256, 512], replicated, may hold values from -0.1875 to 0.1875
- proj_weight: bfloat16 [512, 1280], replicated, may hold values from -0.375 to 0.375
- ln_first: float32 [1280], replicated, may hold values from 0.25 to 1.75
- qkv_weight: bfloat16 [1280, 3, 1280], P('dp', None, 'space'), as said below
- out_weight: bfloat16 [1280, 1280], P('space', 'dp'), may hold values from -0.15625 to 0.15625
- ln_second: float32 [1280], replicated, may hold values from 0.25 to 1.75
- up_weight: bfloat16 [1280, 5120], P('dp', 'space'), may hold values from -0.15625 to 0.15625
- down_weight: bfloat16 [5120, 1280], P('space', 'dp'), may hold values from -0.125 to 0.125
Outputs:
- encoded: bfloat16 [16, 1024, 1280], P('dp', 'space')
Inputs may be any that keep to these rules, and one draw needn't show every extreme that they name: `qkv_weight`: every entry is at most 135 * 1280 ** -0.5 in magnitude.
All inputs are finite; a program needn't handle non-finite values.
Results may differ from a plain program's by a relative error of at most 0.014.
Values may be sent and summed in bfloat16 or wider, within the bound.
A program may use at most 128 MiB of HBM per device.

v0:
```python
import jax
import jax.numpy as jnp
from jax import lax
from jax.sharding import PartitionSpec as P

HEADS = 16


def passed_along(value, axis, steps):
    count = lax.axis_size(axis)
    leading, last = (max(0, -steps), min(count, count - steps))
    return lax.ppermute(value, axis, [(source, source + steps) for source in range(leading, last)])


def conv_rows(image_field, kernel, spec):
    out = lax.conv_general_dilated(
        image_field,
        kernel,
        (2, 2),
        ((0, 0), (1, 1)),
        dimension_numbers=spec,
        preferred_element_type=jnp.float32,
    )
    return jax.nn.relu(out).astype(jnp.bfloat16)


def layer_norm(values, gain):
    wide = values.astype(jnp.float32)
    center = wide - jnp.mean(wide, axis=-1, keepdims=True)
    spread = jnp.mean(center * center, axis=-1, keepdims=True)
    return (center * lax.rsqrt(spread + 1e-06) * gain).astype(jnp.bfloat16)


def attend(query, keys, values):
    head_size = query.shape[-1]
    divisor = jnp.sqrt(jnp.float32(head_size))

    def one_head(items):
        head_query, head_keys, head_values = items
        scores = (
            jnp.einsum("gqd,gkd->gqk", head_query, head_keys, preferred_element_type=jnp.float32)
            / divisor
        )
        weights = jax.nn.softmax(scores, axis=-1).astype(jnp.bfloat16)
        return jnp.einsum(
            "gqk,gkd->gqd", weights, head_values, preferred_element_type=jnp.float32
        ).astype(jnp.bfloat16)

    mixed = lax.map(
        one_head, (jnp.moveaxis(query, 2, 0), jnp.moveaxis(keys, 2, 0), jnp.moveaxis(values, 2, 0))
    )
    return jnp.moveaxis(mixed, 0, 2)


def device_rows(values, start, total, groups, per_device, weight):
    token_start = start // groups
    token_count = total // groups
    slab = lax.dynamic_slice_in_dim(values, token_start, token_count, 1)
    owners = token_count // per_device
    slab = slab.reshape(groups, owners, per_device, values.shape[2])
    slab = jnp.transpose(slab, (1, 0, 2, 3)).reshape(total, values.shape[2])
    return jnp.dot(slab, weight, preferred_element_type=jnp.float32)


def on_device(
    images,
    pos_embed,
    conv_first,
    conv_second,
    conv_third,
    conv_fourth,
    proj_weight,
    ln_first,
    qkv_weight,
    out_weight,
    ln_second,
    up_weight,
    down_weight,
):
    spec_first = ("NCHW", "HWIO", "NHWC")
    spec_later = ("NHWC", "HWIO", "NHWC")
    margin = passed_along(images[:, :, -15:, :], "space", 1)
    stem_out = conv_rows(jnp.concatenate([margin, images], axis=2), conv_first, spec_first)
    for kernel in (conv_second, conv_third, conv_fourth):
        stem_out = conv_rows(stem_out, kernel, spec_later)
    groups, height, across, channels = stem_out.shape
    flat = stem_out.reshape(groups, height * across, channels)
    tokens = (
        jnp.dot(flat, proj_weight, preferred_element_type=jnp.float32)
        + pos_embed.astype(jnp.float32)
    ).astype(jnp.bfloat16)
    qkv_part, out_part = (
        lax.all_gather(qkv_weight, "dp", axis=0, tiled=True),
        lax.all_gather(out_weight, "dp", axis=1, tiled=True),
    )
    width = tokens.shape[2]
    count = tokens.shape[1]
    local = qkv_part.shape[2]
    head_size = width // HEADS
    local_heads = local // head_size
    qkv_matrix = qkv_part.reshape(width, 3 * local)
    qkv_all = jnp.dot(
        layer_norm(lax.all_gather(tokens, "space", axis=1, tiled=True), ln_first),
        qkv_matrix,
        preferred_element_type=jnp.float32,
    ).astype(jnp.bfloat16)
    seen = qkv_all.shape[1]
    qkv_all = qkv_all.reshape(groups, seen, 3, local_heads, head_size)
    mixed = attend(qkv_all[:, :, 0], qkv_all[:, :, 1], qkv_all[:, :, 2]).reshape(
        groups, seen, local
    )
    attn_sum = (
        lax.psum_scatter(
            device_rows(
                mixed,
                jnp.int32(0),
                groups * count * lax.axis_size("space"),
                groups,
                count,
                out_part,
            ).astype(jnp.bfloat16),
            "space",
            scatter_dimension=0,
            tiled=True,
        )
        .astype(jnp.float32)
        .reshape(groups, count, width)
    )
    after_attn = (tokens.astype(jnp.float32) + attn_sum).astype(jnp.bfloat16)
    normed_two = layer_norm(after_attn, ln_second)
    group_rows = lax.all_gather(normed_two, "space", axis=1, tiled=True)
    seen_rows = group_rows.shape[1]
    hidden_cols = up_weight.shape[1]
    start_hidden = jnp.zeros((groups, seen_rows, hidden_cols), jnp.float32)
    before_gelu = start_hidden + jnp.einsum(
        "gtd,df->gtf",
        group_rows,
        lax.all_gather(up_weight, "dp", axis=0, tiled=True),
        preferred_element_type=jnp.float32,
    )
    hidden = jax.nn.gelu(before_gelu, approximate=False).astype(jnp.bfloat16)
    down_part = lax.all_gather(down_weight, "dp", axis=1, tiled=True)
    mlp_sum = (
        lax.psum_scatter(
            device_rows(
                hidden,
                jnp.int32(0),
                groups * count * lax.axis_size("space"),
                groups,
                count,
                down_part,
            ).astype(jnp.bfloat16),
            "space",
            scatter_dimension=0,
            tiled=True,
        )
        .astype(jnp.float32)
        .reshape(groups, count, width)
    )
    return (after_attn.astype(jnp.float32) + mlp_sum).astype(jnp.bfloat16)


def solution(mesh):
    placed = (
        P("dp", None, "space", None),
        P("space", None),
        P(),
        P(),
        P(),
        P(),
        P(),
        P(),
        P("dp", None, "space"),
        P("space", "dp"),
        P(),
        P("dp", "space"),
        P("space", "dp"),
    )
    return jax.shard_map(
        on_device, mesh=mesh, in_specs=placed, out_specs=P("dp", "space", None), check_vma=False
    )
```

profile of v0, /device:TPU:0, one launch (start us, length us, event | category | flops | bytes accessed | tf_op | source)
XLA Modules:
  0.0 586.7 jit_solution(12435895969867735964)
XLA Ops:
  7.5 4.9 collective-permute-start
  15.9 2.9 reshape.228
  18.8 19.6 %copy.46 = bf16[3,271,1,8,66]{3,0,4,1,2:T(4,128)(2,1)} copy(bf16[3,271,1,8,66]{4,3,1,0,2:T(8,128)(2,1)} %reshape.228) | data formatting | bytes 1717056 | tf_op jit(solution)/shard_map/conv_general_dilated | solution.py:16
  39.8 27.8 %fusion.44 = bf16[135,8,33,64]{3,1,2,0:T(8,128)(2,1)} fusion(pred[8,33]{0,1:T(8,128)(4,1)S(1)} %copy-done.8, bf16[3,3,3,64]{3,2,1,0:T(4,128)(2,1)S(1)} %copy-done.6, bf16[3,271,1,7,2]{3,0,4,1,2:T(4,128)(2,1)S(1)} %slice.25, bf16[3,271,1,8,66]{3,0,4,1,2:T(4,128)(2,1)} %copy.46), kind=kOutput, calls=%fused_computation.57 | convolution fusion | flops 134949312 | bytes 5446932 | tf_op jit(solution)/shard_map/conv_general_dilated | solution.py:16
  67.6 16.3 %copy.47 = bf16[135,8,33,64]{0,3,2,1:T(8,128)(2,1)} copy(bf16[135,8,33,64]{3,1,2,0:T(8,128)(2,1)} %fusion.44) | data formatting | bytes 9123840 | tf_op jit(solution)/shard_map/convert_element_type | solution.py:24
  84.0 8.3 %slice.26 = bf16[135,1,256,64]{0,3,2,1:T(8,128)(2,1)} slice(bf16[135,1,264,64]{0,3,2,1:T(8,128)(2,1)} %bitcast.122), slice={[0:135], [0:1], [0:256], [0:64]} | slice | bytes 8847360 | tf_op jit(solution)/shard_map/convert_element_type | solution.py:24
  92.3 15.6 %copy.48 = bf16[135,1,8,32,64]{4,2,3,0,1:T(8,128)(2,1)} copy(bf16[135,1,8,32,64]{0,4,3,2,1:T(8,128)(2,1)} %bitcast.123) | data formatting | bytes 8847360 | tf_op jit(solution)/shard_map/convert_element_type | solution.py:24
  109.1 6.6 %fusion.86 = bf16[67,1,8,16,128]{4,2,3,0,1:T(8,128)(2,1)S(1)} fusion(bf16[3,3,64,128]{3,2,1,0:T(8,128)(2,1)S(1)} %copy-done.5, bf16[135,1,7,1,64]{4,2,3,0,1:T(8,128)(2,1)S(1)} %get-tuple-element.63, bf16[135,1,7,1,64]{4,2,3,0,1:T(8,128)(2,1)S(1)} %get-tuple-element.62, bf16[135,1,8,32,64]{4,2,3,0,1:T(8,128)(2,1)} %copy.48), kind=kOutput, calls=%fused_computation.105 | convolution fusion | flops 1290278912 | bytes 7008512 | tf_op jit(solution)/shard_map/conv_general_dilated | solution.py:16
  119.3 3.7 fusion.63
  124.5 39.7 %all-gather.17.cloned.1.call-done = bf16[1024,1280]{1,0:T(8,128)(2,1)} async-done(((bf16[512,1280]{1,0:T(8,128)(2,1)}), bf16[1024,1280]{1,0:T(8,128)(2,1)}) %all-gather.17.cloned.1.call-update) | async-done | bytes 2621456 | tf_op jit(solution)/shard_map/all_gather | solution.py:103
  169.0 51.6 %all-gather.9.cloned.1.call-done = bf16[1280,3,640]{2,0,1:T(8,128)(2,1)} async-done(((bf16[80,3,640]{2,0,1:T(8,128)(2,1)}), bf16[1280,3,640]{2,0,1:T(8,128)(2,1)}) %all-gather.9.cloned.1.call-update) | async-done | bytes 4915216 | tf_op jit(solution)/shard_map/all_gather | solution.py:93
  220.6 8.2 %copy.52 = bf16[1280,3,640]{0,2,1:T(8,128)(2,1)} copy(bf16[1280,3,640]{2,0,1:T(8,128)(2,1)} %all-gather.9.cloned.1.call-done) | data formatting | bytes 9830400 | tf_op jit(solution)/shard_map/all_gather | solution.py:93
  228.8 10.3 %convolution_convert_fusion.1 = bf16[1024,1920]{1,0:T(8,128)(2,1)} fusion(bf16[1280,1920]{0,1:T(8,128)(2,1)} %bitcast.125, bf16[1024,1280]{1,0:T(8,128)(2,1)} %all-gather.17.cloned.1.call-done, f32[1280]{0:T(1024)S(1)} %copy-done.7, f32[1024]{0:T(1024)S(1)} %add_rsqrt_fusion, f32[1024]{0:T(1024)S(1)} %broadcast_multiply_fusion), kind=kOutput, calls=%fused_computation.78 | convolution fusion | flops 5041684480 | bytes 11482112 | tf_op jit(solution)/shard_map/dot_general | solution.py:102
  239.0 6.3 %copy.53 = bf16[1024,1920]{0,1:T(8,128)(2,1)} copy(bf16[1024,1920]{1,0:T(8,128)(2,1)} %convolution_convert_fusion.1) | data formatting | bytes 7864320 | tf_op jit(solution)/shard_map/convert_element_type | solution.py:106
  245.3 4.2 slice_bitcast_fusion
  249.5 39.8 %while.10 = (s32[]{:T(128)}, bf16[8,1,1024,80]{2,3,1,0:T(8,128)(2,1)}, bf16[8,1,1024,80]{2,3,0,1:T(8,128)(2,1)}, bf16[8,1,1024,80]{2,3,0,1:T(8,128)(2,1)S(1)}, bf16[8,1,1024,80]{2,3,0,1:T(8,128)(2,1)}, /*index=5*/s32[]{:T(128)}) while((s32[]{:T(128)}, bf16[8,1,1024,80]{2,3,1,0:T(8,128)(2,1)}, bf16[8,1,1024,80]{2,3,0,1:T(8,128)(2,1)}, ...), condition=%wide.region_5.6_spmd, body=%wide.region_2.5_spmd.sunk | while | flops 345061376 | bytes 13260869 | solution.py:49
  289.4 5.5 convolution_convert_fusion
  296.2 35.4 %reduce-scatter.3.cloned.1.call-done = bf16[512,1280]{1,0:T(8,128)(2,1)} async-done(((bf16[1024,1280]{1,0:T(8,128)(2,1)}), bf16[512,1280]{1,0:T(8,128)(2,1)}) %reduce-scatter.3.cloned.1.call-update) | async-done | bytes 1310736 | tf_op jit(solution)/shard_map/reduce_scatter | solution.py:113
  336.4 60.2 %all-gather.13.cloned.1.call-done = bf16[1280,2560]{1,0:T(8,128)(2,1)} async-done(((bf16[80,2560]{1,0:T(8,128)(2,1)}), bf16[1280,2560]{1,0:T(8,128)(2,1)}) %all-gather.13.cloned.1.call-update) | async-done | bytes 6553616 | tf_op jit(solution)/shard_map/all_gather | solution.py:138
  396.6 63.7 %all-gather.15.cloned.1.call-done = bf16[2560,1280]{0,1:T(8,128)(2,1)} async-done(((bf16[2560,80]{0,1:T(8,128)(2,1)}), bf16[2560,1280]{0,1:T(8,128)(2,1)}) %all-gather.15.cloned.1.call-update) | async-done | bytes 6553616 | tf_op jit(solution)/shard_map/all_gather | solution.py:142
  460.3 39.3 %all-gather.19.cloned.1.call-done = bf16[1024,1280]{1,0:T(8,128)(2,1)} async-done(((bf16[512,1280]{1,0:T(8,128)(2,1)}), bf16[1024,1280]{1,0:T(8,128)(2,1)}) %all-gather.19.cloned.1.call-update) | async-done | bytes 2621456 | tf_op jit(solution)/shard_map/all_gather | solution.py:131
  499.6 38.9 %fusion.58 = bf16[1024,1280]{1,0:T(8,128)(2,1)} fusion(bf16[2560,1280]{0,1:T(8,128)(2,1)} %all-gather.15.cloned.1.call-done, bf16[1024,1280]{1,0:T(8,128)(2,1)} %all-gather.19.cloned.1.call-done, bf16[1280,2560]{1,0:T(8,128)(2,1)} %all-gather.13.cloned.1.call-done), kind=kOutput, calls=%fused_computation.76 | convolution fusion | flops 13593477120 | bytes 18350080 | tf_op jit(solution)/shard_map/dot_general | solution.py:62
  538.5 37.8 %reduce-scatter.5.cloned.1.call-done = bf16[512,1280]{1,0:T(8,128)(2,1)} async-done(((bf16[1024,1280]{1,0:T(8,128)(2,1)}), bf16[512,1280]{1,0:T(8,128)(2,1)}) %reduce-scatter.5.cloned.1.call-update) | async-done | bytes 1310736 | tf_op jit(solution)/shard_map/reduce_scatter | solution.py:144
  576.4 3.1 fusion.104
  (81 shorter events, 62.6 us)
Async XLA Ops:
  6.5 110.9 %copy-start = (bf16[3,3,256,512]{3,2,1,0:T(8,128)(2,1)S(1)}, bf16[3,3,256,512]{3,2,1,0:T(8,128)(2,1)}, u32[]{:S(2)}) copy-start(bf16[3,3,256,512]{3,2,1,0:T(8,128)(2,1)} %param.20) | copy-start | bytes 7077892
  6.5 157.7 %all-gather.17.cloned.1.call-start = ((), (), s32[]{:S(2)}) async-start(), calls=%async_computation.8 | async-start | bytes 3932160 | tf_op jit(solution)/shard_map/all_gather | solution.py:103
  7.5 6.6 %collective-permute-start = (bf16[1,3,15,512]{3,2,1,0:T(8,128)(2,1)S(1)}, bf16[1,3,15,512]{3,2,1,0:T(8,128)(2,1)S(1)}, u32[]{:S(2)}, u32[]{:S(2)}) collective-permute-start(bf16[1,3,15,512]{3,2,1,0:T(8,128)(2,1)S(1)} %slice.12), channel_id=1, source_target_pairs={{0,1},{2,3},{4,5},{6,7},{8,9},{10,11},{12,13},{14,15},{16,17},{18,... | collective-permute-start | bytes 138248 | tf_op jit(solution)/shard_map/ppermute | solution.py:12
  18.8 21.0 %copy-start.6 = (bf16[3,3,3,64]{3,2,1,0:T(4,128)(2,1)S(1)}, bf16[3,3,3,64]{3,2,1,0:T(4,128)(2,1)}, u32[]{:S(2)}) copy-start(bf16[3,3,3,64]{3,2,1,0:T(4,128)(2,1)} %param.17) | copy-start | bytes 10372
  18.8 21.0 %copy-start.8 = (pred[8,33]{0,1:T(8,128)(4,1)S(1)}, pred[8,33]{0,1:T(8,128)(4,1)}, u32[]{:S(2)}) copy-start(pred[8,33]{0,1:T(8,128)(4,1)} %constant.128) | copy-start | bytes 796
  92.3 16.8 %copy-start.5 = (bf16[3,3,64,128]{3,2,1,0:T(8,128)(2,1)S(1)}, bf16[3,3,64,128]{3,2,1,0:T(8,128)(2,1)}, u32[]{:S(2)}) copy-start(bf16[3,3,64,128]{3,2,1,0:T(8,128)(2,1)} %param.18) | copy-start | bytes 442372
  109.1 6.7 %copy-start.4 = (bf16[3,3,128,256]{3,2,1,0:T(8,128)(2,1)S(1)}, bf16[3,3,128,256]{3,2,1,0:T(8,128)(2,1)}, u32[]{:S(2)}) copy-start(bf16[3,3,128,256]{3,2,1,0:T(8,128)(2,1)} %param.19) | copy-start | bytes 1769476
  123.0 97.6 %all-gather.9.cloned.1.call-start = ((), (), s32[]{:S(2)}) async-start(), calls=%async_computation.2 | async-start | bytes 5222400 | tf_op jit(solution)/shard_map/all_gather | solution.py:93
  123.7 165.7 %all-gather.11.cloned.1.call-start = ((), (), s32[]{:S(2)}) async-start(), calls=%async_computation.3 | async-start | bytes 1740800 | tf_op jit(solution)/shard_map/all_gather | solution.py:94
  124.5 207.1 %reduce-scatter.3.cloned.1.call-start = ((), (), s32[]{:S(2)}) async-start(), calls=%async_computation.4 | async-start | bytes 3932160 | tf_op jit(solution)/shard_map/reduce_scatter | solution.py:113
  169.0 59.8 %copy-start.7 = (f32[1280]{0:T(1024)S(1)}, f32[1280]{0:T(1024)}, u32[]{:S(2)}) copy-start(f32[1280]{0:T(1024)} %param.22) | copy-start | bytes 15364
  294.9 39.9 %copy-start.3 = (f32[1280]{0:T(1024)S(1)}, f32[1280]{0:T(1024)}, u32[]{:S(2)}) copy-start(f32[1280]{0:T(1024)} %param.25) | copy-start | bytes 15364
  295.0 101.6 %all-gather.13.cloned.1.call-start = ((), (), s32[]{:S(2)}) async-start(), calls=%async_computation.5 | async-start | bytes 6963200 | tf_op jit(solution)/shard_map/all_gather | solution.py:138
  295.5 164.8 %all-gather.15.cloned.1.call-start = ((), (), s32[]{:S(2)}) async-start(), calls=%async_computation.6 | async-start | bytes 6963200 | tf_op jit(solution)/shard_map/all_gather | solution.py:142
  296.1 203.5 %all-gather.19.cloned.1.call-start = ((), (), s32[]{:S(2)}) async-start(), calls=%async_computation.9 | async-start | bytes 3932160 | tf_op jit(solution)/shard_map/all_gather | solution.py:131
  333.7 1.1 copy-start.2
  336.3 240.1 %reduce-scatter.5.cloned.1.call-start = ((), (), s32[]{:S(2)}) async-start(), calls=%async_computation.7 | async-start | bytes 3932160 | tf_op jit(solution)/shard_map/reduce_scatter | solution.py:144
  499.6 79.8 %copy-start.1 = (bf16[3,3,256,512]{3,2,1,0:T(8,128)(2,1)S(1)}, bf16[3,3,256,512]{3,2,1,0:T(8,128)(2,1)}, u32[]{:S(2)}) copy-start(bf16[3,3,256,512]{3,2,1,0:T(8,128)(2,1)} %param.20) | copy-start | bytes 7077892
Sparse Core Ops, SparseCore 0:
  123.1 41.0 all-gather.16
  166.4 54.1 all-gather.8
  222.8 38.4 all-gather.10
  295.1 36.4 reduce-scatter.2
  333.7 62.8 all-gather.12
  398.7 61.5 all-gather.14
  461.9 37.7 all-gather.18
  538.7 37.6 reduce-scatter.4
where the time goes:
time: 598 us; the launch traced here: 587 us
  waiting for transfers between devices  332 us (56%)
  matrix products  130 us (22%)
  local copies, waits for them, and re-layouts  86.5 us (14%)
  other arithmetic  19.2 us (3%)
  between operations  14.1 us (2%)
    all_gather x1, waiting for transfers between devices, on_device(): down_part = lax.all_gather(down_weight, 'dp', axis=1, tiled=True)  63.7 us
    all_gather x1, waiting for transfers between devices, on_device(): lax.all_gather(up_weight, 'dp', axis=0, tiled=True)  60.2 us
    all_gather x1, waiting for transfers between devices, on_device(): lax.all_gather(qkv_weight, 'dp', axis=0, tiled=True)  51.6 us
    dot_general x2, matrix products, device_rows(): return jnp.dot(slab, weight, preferred_element_type=jnp.float32)  44.5 us
    convert_element_type x7, local copies, waits for them, and re-layouts, conv_rows(): return jax.nn.relu(out).astype(jnp.bfloat16)  41.8 us
    all_gather x1, waiting for transfers between devices, on_device(): lax.all_gather(tokens, 'space', axis=1, tiled=True)  39.7 us
    all_gather x1, waiting for transfers between devices, on_device(): group_rows = lax.all_gather(normed_two, 'space', axis=1, tiled=True)  39.3 us
    reduce_scatter x1, waiting for transfers between devices, on_device(): lax.psum_scatter(device_rows(hidden, jnp.int32(0), groups * count * lax.a...  37.8 us
  transfers between devices with their start and end apart: 9, of which 8 were waited for; matrix products, arithmetic and copies ran while one was open for 13% of the time, Pallas kernels for 0%

commit v1 on v0

--- a/solution.py
+++ b/solution.py
@@ -139,7 +139,7 @@
         preferred_element_type=jnp.float32,
     )
     hidden = jax.nn.gelu(before_gelu, approximate=False).astype(jnp.bfloat16)
-    down_part = lax.all_gather(down_weight, "dp", axis=1, tiled=True)
+    down_part = jnp.concatenate(lax.all_gather(down_weight, "dp"), axis=1)
     mlp_sum = (
         lax.psum_scatter(
             device_rows(

time: 598 us -> 598 us (level)
  waiting for transfers between devices: 332 us -> 321 us
  local copies, waits for them, and re-layouts: 86.5 us -> 97.4 us
    all_gather x1, waiting for transfers between devices: 60.2 us -> 52.3 us  [on_device(): lax.all_gather(up_weight, 'dp', axis=0, tiled=True)]
    reshape x0 -> x1, local copies, waits for them, and re-layouts: none -> 6.34 us  [on_device(): down_part = jnp.concatenate(lax.all_gather(down_weight, 'dp'), axis=1)]
  transfers between devices with their start and end apart: 9 -> 9, of which waited for: 8 -> 8; matrix products, arithmetic and copies ran while one was open for 13% -> 15% of each run, Pallas kernels for 0% -> 0%
where the time goes in v1:
time: 598 us; the launch traced here: 586 us
  waiting for transfers between devices  321 us (54%)
  matrix products  130 us (22%)
  local copies, waits for them, and re-layouts  97.4 us (16%)
  other arithmetic  19.2 us (3%)
  between operations  13.9 us (2%)
    all_gather x1, waiting for transfers between devices, on_device(): down_part = jnp.concatenate(lax.all_gather(down_weight, 'dp'), axis=1)  60.4 us
    all_gather x1, waiting for transfers between devices, on_device(): lax.all_gather(up_weight, 'dp', axis=0, tiled=True)  52.3 us
    all_gather x1, waiting for transfers between devices, on_device(): lax.all_gather(qkv_weight, 'dp', axis=0, tiled=True)  51.6 us
    dot_general x2, matrix products, device_rows(): return jnp.dot(slab, weight, preferred_element_type=jnp.float32)  44.4 us
    convert_element_type x7, local copies, waits for them, and re-layouts, conv_rows(): return jax.nn.relu(out).astype(jnp.bfloat16)  41.8 us
    all_gather x1, waiting for transfers between devices, on_device(): lax.all_gather(tokens, 'space', axis=1, tiled=True)  39.7 us
    all_gather x1, waiting for transfers between devices, on_device(): group_rows = lax.all_gather(normed_two, 'space', axis=1, tiled=True)  39.3 us
    reduce_scatter x1, waiting for transfers between devices, on_device(): lax.psum_scatter(device_rows(hidden, jnp.int32(0), groups * count * lax.a...  37.8 us
  transfers between devices with their start and end apart: 9, of which 8 were waited for; matrix products, arithmetic and copies ran while one was open for 15% of the time, Pallas kernels for 0%

profile of v1, /device:TPU:0, one launch (start us, length us, event | category | flops | bytes accessed | tf_op | source)
XLA Modules:
  0.0 586.4 jit_solution(17830287785673419937)
XLA Ops:
  7.5 4.9 collective-permute-start
  18.8 19.6 %copy.61 = bf16[3,271,1,8,66]{3,0,4,1,2:T(4,128)(2,1)} copy(bf16[3,271,1,8,66]{4,3,1,0,2:T(8,128)(2,1)} %reshape.237) | data formatting | bytes 1717056 | tf_op jit(solution)/shard_map/conv_general_dilated | solution.py:16
  39.8 27.8 %fusion.44 = bf16[135,8,33,64]{3,1,2,0:T(8,128)(2,1)} fusion(pred[8,33]{0,1:T(8,128)(4,1)S(1)} %copy-done.8, bf16[3,3,3,64]{3,2,1,0:T(4,128)(2,1)S(1)} %copy-done.6, bf16[3,271,1,7,2]{3,0,4,1,2:T(4,128)(2,1)S(1)} %slice.25, bf16[3,271,1,8,66]{3,0,4,1,2:T(4,128)(2,1)} %copy.61), kind=kOutput, calls=%fused_computation.57 | convolution fusion | flops 134949312 | bytes 5446932 | tf_op jit(solution)/shard_map/conv_general_dilated | solution.py:16
  67.6 16.3 %copy.62 = bf16[135,8,33,64]{0,3,2,1:T(8,128)(2,1)} copy(bf16[135,8,33,64]{3,1,2,0:T(8,128)(2,1)} %fusion.44) | data formatting | bytes 9123840 | tf_op jit(solution)/shard_map/convert_element_type | solution.py:24
  84.0 8.3 %slice.26 = bf16[135,1,256,64]{0,3,2,1:T(8,128)(2,1)} slice(bf16[135,1,264,64]{0,3,2,1:T(8,128)(2,1)} %bitcast.129), slice={[0:135], [0:1], [0:256], [0:64]} | slice | bytes 8847360 | tf_op jit(solution)/shard_map/convert_element_type | solution.py:24
  92.3 15.6 %copy.63 = bf16[135,1,8,32,64]{4,2,3,0,1:T(8,128)(2,1)} copy(bf16[135,1,8,32,64]{0,4,3,2,1:T(8,128)(2,1)} %bitcast.130) | data formatting | bytes 8847360 | tf_op jit(solution)/shard_map/convert_element_type | solution.py:24
  109.1 6.6 %fusion.86 = bf16[67,1,8,16,128]{4,2,3,0,1:T(8,128)(2,1)S(1)} fusion(bf16[3,3,64,128]{3,2,1,0:T(8,128)(2,1)S(1)} %copy-done.5, bf16[135,1,7,1,64]{4,2,3,0,1:T(8,128)(2,1)S(1)} %get-tuple-element.68, bf16[135,1,7,1,64]{4,2,3,0,1:T(8,128)(2,1)S(1)} %get-tuple-element.67, bf16[135,1,8,32,64]{4,2,3,0,1:T(8,128)(2,1)} %copy.63), kind=kOutput, calls=%fused_computation.105 | convolution fusion | flops 1290278912 | bytes 7008512 | tf_op jit(solution)/shard_map/conv_general_dilated | solution.py:16
  119.3 3.7 fusion.63
  124.5 39.7 %all-gather.16.cloned.1.call-done = bf16[1024,1280]{1,0:T(8,128)(2,1)} async-done(((bf16[512,1280]{1,0:T(8,128)(2,1)}), bf16[1024,1280]{1,0:T(8,128)(2,1)}) %all-gather.16.cloned.1.call-update) | async-done | bytes 2621456 | tf_op jit(solution)/shard_map/all_gather | solution.py:103
  169.0 51.6 %all-gather.10.cloned.1.call-done = bf16[1280,3,640]{2,0,1:T(8,128)(2,1)} async-done(((bf16[80,3,640]{2,0,1:T(8,128)(2,1)}), bf16[1280,3,640]{2,0,1:T(8,128)(2,1)}) %all-gather.10.cloned.1.call-update) | async-done | bytes 4915216 | tf_op jit(solution)/shard_map/all_gather | solution.py:93
  220.6 8.2 %copy.67 = bf16[1280,3,640]{0,2,1:T(8,128)(2,1)} copy(bf16[1280,3,640]{2,0,1:T(8,128)(2,1)} %all-gather.10.cloned.1.call-done) | data formatting | bytes 9830400 | tf_op jit(solution)/shard_map/all_gather | solution.py:93
  228.8 10.3 %convolution_convert_fusion.1 = bf16[1024,1920]{1,0:T(8,128)(2,1)} fusion(bf16[1280,1920]{0,1:T(8,128)(2,1)} %bitcast.135, bf16[1024,1280]{1,0:T(8,128)(2,1)} %all-gather.16.cloned.1.call-done, f32[1280]{0:T(1024)S(1)} %copy-done.7, f32[1024]{0:T(1024)S(1)} %add_rsqrt_fusion, f32[1024]{0:T(1024)S(1)} %broadcast_multiply_fusion), kind=kOutput, calls=%fused_computation.78 | convolution fusion | flops 5041684480 | bytes 11482112 | tf_op jit(solution)/shard_map/dot_general | solution.py:102
  239.0 6.3 %copy.68 = bf16[1024,1920]{0,1:T(8,128)(2,1)} copy(bf16[1024,1920]{1,0:T(8,128)(2,1)} %convolution_convert_fusion.1) | data formatting | bytes 7864320 | tf_op jit(solution)/shard_map/convert_element_type | solution.py:106
  245.3 4.2 slice_bitcast_fusion
  249.5 39.8 %while.10 = (s32[]{:T(128)}, bf16[8,1,1024,80]{2,3,1,0:T(8,128)(2,1)}, bf16[8,1,1024,80]{2,3,0,1:T(8,128)(2,1)}, bf16[8,1,1024,80]{2,3,0,1:T(8,128)(2,1)S(1)}, bf16[8,1,1024,80]{2,3,0,1:T(8,128)(2,1)}, /*index=5*/s32[]{:T(128)}) while((s32[]{:T(128)}, bf16[8,1,1024,80]{2,3,1,0:T(8,128)(2,1)}, bf16[8,1,1024,80]{2,3,0,1:T(8,128)(2,1)}, ...), condition=%wide.region_5.6_spmd, body=%wide.region_2.5_spmd.sunk | while | flops 345061376 | bytes 13260869 | solution.py:49
  289.4 5.5 convolution_convert_fusion
  296.2 35.4 %reduce-scatter.3.cloned.1.call-done = bf16[512,1280]{1,0:T(8,128)(2,1)} async-done(((bf16[1024,1280]{1,0:T(8,128)(2,1)}), bf16[512,1280]{1,0:T(8,128)(2,1)}) %reduce-scatter.3.cloned.1.call-update) | async-done | bytes 1310736 | tf_op jit(solution)/shard_map/reduce_scatter | solution.py:113
  336.2 60.4 %all-gather.20.cloned.1.call-done = bf16[40960,80]{0,1:T(8,128)(2,1)} async-done(((bf16[2560,80]{0,1:T(8,128)(2,1)}), bf16[40960,80]{0,1:T(8,128)(2,1)}) %all-gather.20.cloned.1.call-update) | async-done | bytes 6553616 | tf_op jit(solution)/shard_map/all_gather | solution.py:142
  396.6 5.1 copy.78
  401.7 6.3 %copy.72 = bf16[2560,16,80]{0,2,1:T(8,128)(2,1)} copy(bf16[2560,16,80]{0,1,2:T(8,128)(2,1)S(1)} %bitcast.131) | data formatting | bytes 13107200 | tf_op jit(solution)/shard_map/reshape | solution.py:142
  408.1 52.3 %all-gather.14.cloned.1.call-done = bf16[1280,2560]{1,0:T(8,128)(2,1)} async-done(((bf16[80,2560]{1,0:T(8,128)(2,1)}), bf16[1280,2560]{1,0:T(8,128)(2,1)}) %all-gather.14.cloned.1.call-update) | async-done | bytes 6553616 | tf_op jit(solution)/shard_map/all_gather | solution.py:138
  460.3 39.3 %all-gather.18.cloned.1.call-done = bf16[1024,1280]{1,0:T(8,128)(2,1)} async-done(((bf16[512,1280]{1,0:T(8,128)(2,1)}), bf16[1024,1280]{1,0:T(8,128)(2,1)}) %all-gather.18.cloned.1.call-update) | async-done | bytes 2621456 | tf_op jit(solution)/shard_map/all_gather | solution.py:131
  499.6 38.9 %fusion.58 = bf16[1024,1280]{1,0:T(8,128)(2,1)} fusion(bf16[2560,1280]{0,1:T(8,128)(2,1)} %bitcast.134, bf16[1024,1280]{1,0:T(8,128)(2,1)} %all-gather.18.cloned.1.call-done, bf16[1280,2560]{1,0:T(8,128)(2,1)} %all-gather.14.cloned.1.call-done), kind=kOutput, calls=%fused_computation.76 | convolution fusion | flops 13593477120 | bytes 18350080 | tf_op jit(solution)/shard_map/dot_general | solution.py:62
  538.5 37.8 %reduce-scatter.5.cloned.1.call-done = bf16[512,1280]{1,0:T(8,128)(2,1)} async-done(((bf16[1024,1280]{1,0:T(8,128)(2,1)}), bf16[512,1280]{1,0:T(8,128)(2,1)}) %reduce-scatter.5.cloned.1.call-update) | async-done | bytes 1310736 | tf_op jit(solution)/shard_map/reduce_scatter | solution.py:144
  (83 shorter events, 68.4 us)
Async XLA Ops:
  6.5 110.9 %copy-start = (bf16[3,3,256,512]{3,2,1,0:T(8,128)(2,1)S(1)}, bf16[3,3,256,512]{3,2,1,0:T(8,128)(2,1)}, u32[]{:S(2)}) copy-start(bf16[3,3,256,512]{3,2,1,0:T(8,128)(2,1)} %param.20) | copy-start | bytes 7077892
  6.5 157.7 %all-gather.16.cloned.1.call-start = ((), (), s32[]{:S(2)}) async-start(), calls=%async_computation.7 | async-start | bytes 3932160 | tf_op jit(solution)/shard_map/all_gather | solution.py:103
  7.5 6.6 %collective-permute-start = (bf16[1,3,15,512]{3,2,1,0:T(8,128)(2,1)S(1)}, bf16[1,3,15,512]{3,2,1,0:T(8,128)(2,1)S(1)}, u32[]{:S(2)}, u32[]{:S(2)}) collective-permute-start(bf16[1,3,15,512]{3,2,1,0:T(8,128)(2,1)S(1)} %slice.12), channel_id=1, source_target_pairs={{0,1},{2,3},{4,5},{6,7},{8,9},{10,11},{12,13},{14,15},{16,17},{18,... | collective-permute-start | bytes 138248 | tf_op jit(solution)/shard_map/ppermute | solution.py:12
  18.8 21.0 %copy-start.6 = (bf16[3,3,3,64]{3,2,1,0:T(4,128)(2,1)S(1)}, bf16[3,3,3,64]{3,2,1,0:T(4,128)(2,1)}, u32[]{:S(2)}) copy-start(bf16[3,3,3,64]{3,2,1,0:T(4,128)(2,1)} %param.17) | copy-start | bytes 10372
  18.8 21.0 %copy-start.8 = (pred[8,33]{0,1:T(8,128)(4,1)S(1)}, pred[8,33]{0,1:T(8,128)(4,1)}, u32[]{:S(2)}) copy-start(pred[8,33]{0,1:T(8,128)(4,1)} %constant.128) | copy-start | bytes 796
  92.3 16.8 %copy-start.5 = (bf16[3,3,64,128]{3,2,1,0:T(8,128)(2,1)S(1)}, bf16[3,3,64,128]{3,2,1,0:T(8,128)(2,1)}, u32[]{:S(2)}) copy-start(bf16[3,3,64,128]{3,2,1,0:T(8,128)(2,1)} %param.18) | copy-start | bytes 442372
  109.1 6.7 %copy-start.4 = (bf16[3,3,128,256]{3,2,1,0:T(8,128)(2,1)S(1)}, bf16[3,3,128,256]{3,2,1,0:T(8,128)(2,1)}, u32[]{:S(2)}) copy-start(bf16[3,3,128,256]{3,2,1,0:T(8,128)(2,1)} %param.19) | copy-start | bytes 1769476
  123.0 97.6 %all-gather.10.cloned.1.call-start = ((), (), s32[]{:S(2)}) async-start(), calls=%async_computation.2 | async-start | bytes 5222400 | tf_op jit(solution)/shard_map/all_gather | solution.py:93
  123.7 165.6 %all-gather.12.cloned.1.call-start = ((), (), s32[]{:S(2)}) async-start(), calls=%async_computation.3 | async-start | bytes 1740800 | tf_op jit(solution)/shard_map/all_gather | solution.py:94
  124.5 207.1 %reduce-scatter.3.cloned.1.call-start = ((), (), s32[]{:S(2)}) async-start(), calls=%async_computation.4 | async-start | bytes 3932160 | tf_op jit(solution)/shard_map/reduce_scatter | solution.py:113
  168.9 59.8 %copy-start.7 = (f32[1280]{0:T(1024)S(1)}, f32[1280]{0:T(1024)}, u32[]{:S(2)}) copy-start(f32[1280]{0:T(1024)} %param.22) | copy-start | bytes 15364
  294.9 39.3 %copy-start.3 = (f32[1280]{0:T(1024)S(1)}, f32[1280]{0:T(1024)}, u32[]{:S(2)}) copy-start(f32[1280]{0:T(1024)} %param.25) | copy-start | bytes 15364
  295.0 101.6 %all-gather.20.cloned.1.call-start = ((), (), s32[]{:S(2)}) async-start(), calls=%async_computation.9 | async-start | bytes 6963200 | tf_op jit(solution)/shard_map/all_gather | solution.py:142
  295.5 164.8 %all-gather.14.cloned.1.call-start = ((), (), s32[]{:S(2)}) async-start(), calls=%async_computation.5 | async-start | bytes 6963200 | tf_op jit(solution)/shard_map/all_gather | solution.py:138
  296.1 203.5 %all-gather.18.cloned.1.call-start = ((), (), s32[]{:S(2)}) async-start(), calls=%async_computation.8 | async-start | bytes 3932160 | tf_op jit(solution)/shard_map/all_gather | solution.py:131
  333.7 68.0 %copy-start.2 = (bf16[512,1280]{1,0:T(8,128)(2,1)}, bf16[512,1280]{1,0:T(8,128)(2,1)S(1)}, u32[]{:S(2)}) copy-start(bf16[512,1280]{1,0:T(8,128)(2,1)S(1)} %get-tuple-element.64) | copy-start | bytes 3932164
  335.8 240.6 %reduce-scatter.5.cloned.1.call-start = ((), (), s32[]{:S(2)}) async-start(), calls=%async_computation.6 | async-start | bytes 3932160 | tf_op jit(solution)/shard_map/reduce_scatter | solution.py:144
  499.6 79.8 %copy-start.1 = (bf16[3,3,256,512]{3,2,1,0:T(8,128)(2,1)S(1)}, bf16[3,3,256,512]{3,2,1,0:T(8,128)(2,1)}, u32[]{:S(2)}) copy-start(bf16[3,3,256,512]{3,2,1,0:T(8,128)(2,1)} %param.20) | copy-start | bytes 7077892
Sparse Core Ops, SparseCore 0:
  123.1 41.0 all-gather.15
  166.4 54.1 all-gather.9
  222.8 38.4 all-gather.11
  295.1 36.4 reduce-scatter.2
  333.7 62.8 all-gather.19
  398.7 61.5 all-gather.13
  461.9 37.7 all-gather.17
  538.6 37.6 reduce-scatter.4
